TPU v7x, 32 devices: a whole 2x2x4 slice. The times are simulated.
32 devices in a mesh: dp: 8 (over z, y), mp: 4 (over x, core).
Axes of the slice: x: 2, y: 2, z: 4, core: 2. Of those that a mesh axis runs over, the one named last changes fastest.
Arguments:
- gradient: bfloat16 [8, 64, 14336], P('dp', None, 'mp'), may hold values from -6 to 6
- momentum: float32 [8, 64, 14336], P('dp', None, 'mp'), may hold values from -6 to 6
- weights: float32 [64, 14336], P(None, 'mp'), may hold values from -6 to 6
- positions: int32 [8, 1, 224, 32], P('dp', None, 'mp'), may hold values from 0 to 4095, as said below
Outputs:
- new_momentum: float32 [8, 64, 14336], P('dp', None, 'mp')
- new_weights: float32 [64, 14336], P(None, 'mp')
Inputs may be any that keep to these rules, and one draw needn't show every extreme that they name: Within one span of one replica the 32 positions are all different.
All inputs are finite; a program needn't handle non-finite values.
Results may differ from a plain program's by a relative error of at most 0.0003.
Values sent between devices are 32-bit elements; how exact they have to be, the bound alone decides.
No kernel may reach another device: no remote copies, remote signals or barrier semaphores. Data moves between devices by JAX's collectives and lax.ppermute only.
A program may use at most 64 MiB of HBM per device.

v0:
```python
import math
import jax
import jax.numpy as jnp
from jax import lax
from jax.sharding import PartitionSpec as P

FF = 14336


def dct_table():
    column = jnp.arange(64, dtype=jnp.float32)
    freq = column[:, None]
    factor = jnp.where(freq == 0, jnp.sqrt(jnp.float32(1.0 / 64)), jnp.sqrt(jnp.float32(2.0 / 64)))
    return factor * jnp.cos(jnp.pi * (2.0 * column[None, :] + 1.0) * freq / 128.0)


def paired_table(table):
    ident = jnp.eye(2, dtype=jnp.float32)
    return (ident[:, None, :, None] * table[None, :, None, :]).reshape(128, 128)


def forward_dct(field, table, paired):
    bands, height, width = field.shape
    along = jnp.einsum("kr,brf->bkf", table, field, precision=lax.Precision.HIGHEST)
    grouped = along.reshape(bands, height, width // 128, 128)
    result = jnp.einsum("bkgs,ls->bkgl", grouped, paired, precision=lax.Precision.HIGHEST)
    return result.reshape(bands, height, width)


def inverse_dct(coefs, table, paired):
    bands, height, width = coefs.shape
    grouped = coefs.reshape(bands, height, width // 128, 128)
    across = jnp.einsum("bkgl,ls->bkgs", grouped, paired, precision=lax.Precision.HIGHEST)
    across = across.reshape(bands, height, width)
    return jnp.einsum("kr,bkf->brf", table, across, precision=lax.Precision.HIGHEST)


def to_spans(field):
    bands, height, width = field.shape
    split = field.reshape(bands, 64, width // 64, 64)
    return jnp.transpose(split, (0, 2, 1, 3))


def from_spans(spans):
    bands, count, height, width = spans.shape
    return jnp.transpose(spans, (0, 2, 1, 3)).reshape(bands, 64, count * 64)


def decode_group(values, places):
    freqs = jnp.arange(64, dtype=jnp.int32)
    row_hot = (places[..., None] // 64 == freqs).astype(jnp.float32) * values[..., None]
    col_hot = (places[..., None] % 64 == freqs).astype(jnp.float32)
    return jnp.einsum("nbcjk,nbcjl->bckl", row_hot, col_hot, precision=lax.Precision.HIGHEST)


def decode_lists(values, places):
    count = values.shape[0]
    group = math.gcd(count, 8)
    steps = count // group
    if steps == 1:
        return decode_group(values, places)

    def add_group(index, total):
        part_values = lax.dynamic_slice_in_dim(values, index * group, group, 0)
        part_places = lax.dynamic_slice_in_dim(places, index * group, group, 0)
        return total + decode_group(part_values, part_places)

    start = jnp.zeros((values.shape[1], values.shape[2], 64, 64), jnp.float32)
    return lax.fori_loop(0, steps, add_group, start)


def local(gradient, momentum, weights, positions):
    table = dct_table()
    paired = paired_table(table)
    summed = 0.9 * momentum[0] + gradient[0].astype(jnp.float32)
    bands = summed.shape[0] // 64
    count = summed.shape[1] // 64
    coefs = forward_dct(summed.reshape(bands, 64, summed.shape[1]), table, paired)
    flattened = to_spans(coefs).reshape(bands, count, 4096)
    own_places = positions[0]
    picked = jnp.take_along_axis(flattened, own_places, axis=2)
    own = decode_group(picked[None], own_places[None])
    back = inverse_dct(from_spans(own), table, paired)
    new_momentum = (summed - back.reshape(summed.shape))[None]
    aggregate = decode_lists(
        lax.all_gather(picked[None], "dp", axis=0, tiled=True),
        lax.all_gather(own_places[None].astype(jnp.float32), "dp", axis=0, tiled=True).astype(
            jnp.int32
        ),
    )
    update = inverse_dct(from_spans(aggregate), table, paired).reshape(weights.shape)
    total_sq = lax.psum(jnp.sum(update * update), "mp")
    meansq = total_sq / (weights.shape[0] * FF)
    new_weights = weights - update / jnp.sqrt(meansq + 1.0)
    return (new_momentum, new_weights)


def solution(mesh):
    placed = (P("dp", None, "mp"), P("dp", None, "mp"), P(None, "mp"), P("dp", None, "mp", None))
    return jax.shard_map(
        local,
        mesh=mesh,
        in_specs=placed,
        out_specs=(P("dp", None, "mp"), P(None, "mp")),
        check_vma=False,
    )
```

profile of v0, /device:TPU:0, one launch (start us, length us, event | category | flops | bytes accessed | tf_op | source)
XLA Modules:
  0.0 132.9 jit_solution(11840959320905657482)
XLA Ops:
  0.7 0.8 fusion.34
  1.7 0.7 convert_element_type.28
  2.4 0.8 copy.30
  3.6 32.3 %all_gather.6 = f32[8,1,56,32]{2,3,1,0:T(8,128)S(1)} all-gather(f32[1,1,56,32]{2,3,1,0:T(8,128)S(1)} %convert_element_type.28), channel_id=1, replica_groups=mesh['dp'=8,'mp'=4] {'dp'}, dimensions={0}, use_global_device_ids=true | all-gather | bytes 64512 | tf_op jit(solution)/shard_map/all_gather | solution.py:87
  36.0 0.8 copy.38
  36.9 0.8 copy.44
  37.7 1.2 convolution_bitcast_fusion.1
  39.1 1.5 %fusion.18 = f32[64,28,128]{2,0,1:T(8,128)S(1)} fusion(f32[128,128,1]{1,0,2:T(8,128)S(1)} %reshape.454, f32[64,28,128]{2,1,0:T(8,128)S(1)} %reshape.436), kind=kOutput, calls=%fused_computation.25 | convolution fusion | flops 352321536 | bytes 1900544 | tf_op jit(solution)/shard_map/bkgs,ls->bkgl/dot_general | solution.py:26
  40.5 0.5 copy.32
  41.1 0.3 reshape_reshape.2
  41.4 1.6 %copy.33 = f32[1,56,64,64]{3,2,1,0:T(8,128)} copy(f32[1,56,64,64]{3,1,2,0:T(8,128)S(1)} %bitcast.113) | data formatting | bytes 1835008 | tf_op jit(solution)/shard_map/transpose | solution.py:41
  43.0 2.1 %reshape.442 = f32[56,4096]{1,0:T(8,128)S(1)} reshape(f32[1,56,64,64]{3,2,1,0:T(8,128)} %copy.33) | data formatting | bytes 1835008 | tf_op jit(solution)/shard_map/reshape | solution.py:79
  45.1 14.0 %gather_fusion = f32[1792]{0:T(1024)S(1)} fusion(f32[56,4096]{1,0:T(8,128)S(1)} %reshape.442, s32[1792]{0:T(1024)S(1)} %reshape.444), kind=kCustom, calls=%fused_computation | custom fusion | bytes 28672 | tf_op jit(solution)/shard_map/jit(take_along_axis)/gather | solution.py:81
  59.3 30.5 %all_gather.7 = f32[8,1,56,32]{2,3,1,0:T(8,128)S(1)} all-gather(f32[1,1,56,32]{2,3,1,0:T(8,128)S(1)} %copy.42), channel_id=1, replica_groups=mesh['dp'=8,'mp'=4] {'dp'}, dimensions={0}, use_global_device_ids=true | all-gather | bytes 64512 | tf_op jit(solution)/shard_map/all_gather | solution.py:86
  90.0 22.1 %fusion.7 = f32[1,64,56,64]{3,1,2,0:T(8,128)S(1)} fusion(s32[8,56,32]{2,0,1:T(8,128)S(1)} %copy-done.5, f32[8,56,32]{2,0,1:T(8,128)S(1)} %copy.43, s32[8,56,32]{2,0,1:T(8,128)S(1)} %copy-done.4), kind=kOutput, calls=%fused_computation.13 | convolution fusion | flops 707395584 | bytes 1089536 | tf_op jit(solution)/shard_map/nbcjk,nbcjl->bckl/dot_general | solution.py:53
  112.1 1.1 copy.45
  113.5 1.5 %convolution_bitcast_fusion.3 = f32[28,8,8,128]{3,2,1,0:T(8,128)S(1)} fusion(f32[128,128,1]{1,0,2:T(8,128)S(1)} %reshape.454, f32[64,28,128]{2,1,0:T(8,128)S(1)} %reshape.440), kind=kOutput, calls=%fused_computation.14 | convolution fusion | flops 352321536 | bytes 1900544 | tf_op jit(solution)/shard_map/bkgl,ls->bkgs/dot_general | solution.py:33
  114.9 1.8 %multiply_reduce_fusion = (f32[]{:T(128)}, f32[3584,64]{0,1:T(8,128)S(1)}) fusion(f32[64]{0:T(128)S(1)} %get-tuple-element.9, f32[64]{0:T(128)S(1)} %get-tuple-element.8, f32[28,8,8,128]{3,2,1,0:T(8,128)S(1)} %convolution_bitcast_fusion.3), kind=kOutput, calls=%fused_computation.27 | convolution fusion | flops 176631808 | bytes 1835524 | tf_op jit(solution)/shard_map/kr,bkf->brf/dot_general | solution.py:35
  116.7 6.4 %psum.7 = f32[]{:T(128)} all-reduce(f32[]{:T(128)} %get-tuple-element.6), channel_id=1, replica_groups=mesh['dp'=8,'mp'=4] {'mp'}, use_global_device_ids=true, to_apply=%region_1.2 | all-reduce | flops 1 | bytes 8 | tf_op jit(solution)/shard_map/psum | solution.py:92
  123.9 1.0 bitcast_subtract_fusion
  124.9 3.1 %convolution_bitcast_fusion.2 = f32[1,64,56,64]{3,1,2,0:T(8,128)S(1)} fusion(s32[56,32]{1,0:T(8,128)S(1)} %get-tuple-element.5, f32[56,32]{1,0:T(8,128)S(1)} %and_select_fusion.1, s32[56,32]{1,0:T(8,128)S(1)} %get-tuple-element.4), kind=kOutput, calls=%fused_computation.12 | convolution fusion | flops 88424448 | bytes 939008 | tf_op jit(solution)/shard_map/nbcjk,nbcjl->bckl/dot_general | solution.py:53
  127.9 1.1 copy.35
  129.3 1.5 %convolution_bitcast_fusion.4 = f32[28,8,8,128]{3,2,1,0:T(8,128)S(1)} fusion(f32[128,128,1]{1,0,2:T(8,128)S(1)} %reshape.454, f32[64,28,128]{2,1,0:T(8,128)S(1)} %reshape.438), kind=kOutput, calls=%fused_computation.15 | convolution fusion | flops 352321536 | bytes 1900544 | tf_op jit(solution)/shard_map/bkgl,ls->bkgs/dot_general | solution.py:33
  130.8 2.0 %fusion.2 = f32[1,64,3584]{2,1,0:T(8,128)} fusion(f32[28,8,8,128]{3,2,1,0:T(8,128)S(1)} %convolution_bitcast_fusion.4, bf16[1,64,3584]{2,1,0:T(8,128)(2,1)S(1)} %copy-done.2, f32[1,64,3584]{2,1,0:T(8,128)S(1)} %copy-done.1, f32[64]{0:T(128)S(1)} %get-tuple-element.9, f32[64]{0:T(128)S(1)} %get-tuple-element.8), kind=kOutput, calls=%fused_computation.7 | convolution fusion | flops 177090560 | bytes 3211776 | tf_op jit(solution)/shard_map/kr,bkf->brf/dot_general | solution.py:35
  (30 shorter events, 1.9 us)
Async XLA Ops:
  0.6 37.0 %copy-start = (f32[1,64,3584]{2,1,0:T(8,128)S(1)}, f32[1,64,3584]{2,1,0:T(8,128)}, u32[]{:S(2)}) copy-start(f32[1,64,3584]{2,1,0:T(8,128)} %param.5) | copy-start | bytes 2752516
  0.6 37.0 %copy-start.2 = (bf16[1,64,3584]{2,1,0:T(8,128)(2,1)S(1)}, bf16[1,64,3584]{2,1,0:T(8,128)(2,1)}, u32[]{:S(2)}) copy-start(bf16[1,64,3584]{2,1,0:T(8,128)(2,1)} %param.4) | copy-start | bytes 1376260
  45.1 44.9 %copy-start.4 = (s32[8,56,32]{2,0,1:T(8,128)S(1)}, s32[8,56,32]{2,0,1:T(8,128)}, u32[]{:S(2)}) copy-start(s32[8,56,32]{2,0,1:T(8,128)} %copy.38) | copy-start | bytes 172036
  45.1 44.9 %copy-start.5 = (s32[8,56,32]{2,0,1:T(8,128)S(1)}, s32[8,56,32]{2,0,1:T(8,128)}, u32[]{:S(2)}) copy-start(s32[8,56,32]{2,0,1:T(8,128)} %copy.44) | copy-start | bytes 172036
  114.9 8.9 %copy-start.3 = (f32[64,3584]{1,0:T(8,128)S(1)}, f32[64,3584]{1,0:T(8,128)}, u32[]{:S(2)}) copy-start(f32[64,3584]{1,0:T(8,128)} %param.6) | copy-start | bytes 2752516
  129.3 1.5 %copy-start.1 = (f32[1,64,3584]{2,1,0:T(8,128)S(1)}, f32[1,64,3584]{2,1,0:T(8,128)}, u32[]{:S(2)}) copy-start(f32[1,64,3584]{2,1,0:T(8,128)} %param.5) | copy-start | bytes 2752516
where the time goes:
time: 133 us
  blocking collectives  69.3 us (52%)
  matrix products  34.5 us (26%)
  local copies, waits for them, and re-layouts  24.5 us (18%)
  other arithmetic  3.01 us (2%)
  between operations  1.57 us (1%)
    all_gather x1, blocking collectives, local(): lax.all_gather(own_places[None].astype(jnp.float32), 'dp', axis=0, tiled=...  32.3 us
    all_gather x1, blocking collectives, local(): lax.all_gather(picked[None], 'dp', axis=0, tiled=True)  30.5 us
    dot_general x2, matrix products, decode_group(): jnp.einsum('nbcjk,nbcjl->bckl', row_hot, col_hot, precision=lax.Precision...  25.1 us
    gather x5, local copies, waits for them, and re-layouts, local(): picked = jnp.take_along_axis(flattened, own_places, axis=2)  14.3 us
    psum x1, blocking collectives, local(): total_sq = lax.psum(jnp.sum(update * update), 'mp')  6.45 us
    dot_general x2, matrix products, inverse_dct(): jnp.einsum('kr,bkf->brf', table, across, precision=lax.Precision.HIGHEST)  3.8 us
    dot_general x2, matrix products, inverse_dct(): jnp.einsum('bkgl,ls->bkgs', grouped, paired, precision=lax.Precision.HIGH...  2.93 us

commit v1 on v0

--- a/solution.py
+++ b/solution.py
@@ -83,7 +83,9 @@
     back = inverse_dct(from_spans(own), table, paired)
     new_momentum = (summed - back.reshape(summed.shape))[None]
     aggregate = decode_lists(
-        lax.all_gather(picked[None], "dp", axis=0, tiled=True),
+        jnp.concatenate(
+            lax.all_to_all(jnp.stack([picked[None]] * lax.axis_size("dp")), "dp", 0, 0), axis=0
+        ),
         lax.all_gather(own_places[None].astype(jnp.float32), "dp", axis=0, tiled=True).astype(
             jnp.int32
         ),

time: 133 us -> 111 us (0.83)
  blocking collectives: 69.3 us -> 37.5 us
  starting transfers between devices: 0 us -> 7.31 us
    all_gather x1 -> x0, blocking collectives: 30.5 us -> none  [local(): lax.all_gather(picked[None], 'dp', axis=0, tiled=True)]
    all_to_all x0 -> x1, starting transfers between devices: none -> 7.31 us  [local(): lax.all_to_all(jnp.stack([picked[None]] * lax.axis_size('dp')), 'dp', 0, 0)]
    all_to_all x0 -> x1, other arithmetic: none -> 1.6 us  [local(): lax.all_to_all(jnp.stack([picked[None]] * lax.axis_size('dp')), 'dp', 0, 0)]
  transfers between devices with their start and end apart: 0 -> 1, of which waited for: 0 -> 0; matrix products, arithmetic and copies ran while one was open for 0% -> 8% of each run, Pallas kernels for 0% -> 0%
where the time goes in v1:
time: 111 us
  blocking collectives  37.5 us (34%)
  matrix products  35.8 us (32%)
  local copies, waits for them, and re-layouts  24.6 us (22%)
  starting transfers between devices  7.31 us (7%)
  other arithmetic  3.79 us (3%)
  between operations  1.61 us (1%)
    all_gather x1, blocking collectives, local(): lax.all_gather(own_places[None].astype(jnp.float32), 'dp', axis=0, tiled=...  31.2 us
    dot_general x2, matrix products, decode_group(): jnp.einsum('nbcjk,nbcjl->bckl', row_hot, col_hot, precision=lax.Precision...  25.2 us
    gather x5, local copies, waits for them, and re-layouts, local(): picked = jnp.take_along_axis(flattened, own_places, axis=2)  14.3 us
    all_to_all x1, starting transfers between devices, local(): lax.all_to_all(jnp.stack([picked[None]] * lax.axis_size('dp')), 'dp', 0, 0)  7.31 us
    psum x1, blocking collectives, local(): total_sq = lax.psum(jnp.sum(update * update), 'mp')  6.27 us
    dot_general x2, matrix products, inverse_dct(): jnp.einsum('kr,bkf->brf', table, across, precision=lax.Precision.HIGHEST)  3.78 us
    dot_general x2, matrix products, inverse_dct(): jnp.einsum('bkgl,ls->bkgs', grouped, paired, precision=lax.Precision.HIGH...  2.92 us
    dot_general x1, matrix products, forward_dct(): jnp.einsum('kr,brf->bkf', table, field, precision=lax.Precision.HIGHEST)  2.51 us
  transfers between devices with their start and end apart: 1, of which 0 were waited for; matrix products, arithmetic and copies ran while one was open for 8% of the time, Pallas kernels for 0%

profile of v1, /device:TPU:0, one launch (start us, length us, event | category | flops | bytes accessed | tf_op | source)
XLA Modules:
  0.0 110.6 jit_solution(11382678414426825892)
XLA Ops:
  0.7 0.7 fusion.34
  1.4 0.8 copy.29
  2.7 2.5 %convolution_bitcast_fusion.1 = f32[1,64,3584]{2,1,0:T(8,128)S(1)} fusion(bf16[1,64,3584]{2,1,0:T(8,128)(2,1)} %param.4, f32[1,64,3584]{2,1,0:T(8,128)} %param.5, f32[64]{0:T(128)S(1)} %get-tuple-element.9, f32[64]{0:T(128)S(1)} %get-tuple-element.8), kind=kOutput, calls=%fused_computation.6 | convolution fusion | flops 176861184 | bytes 2294272 | tf_op jit(solution)/shard_map/kr,brf->bkf/dot_general | solution.py:24
  5.4 1.5 %fusion.18 = f32[64,28,128]{2,0,1:T(8,128)S(1)} fusion(f32[128,128,1]{1,0,2:T(8,128)S(1)} %reshape.463, f32[64,28,128]{2,1,0:T(8,128)S(1)} %reshape.445), kind=kOutput, calls=%fused_computation.25 | convolution fusion | flops 352321536 | bytes 1900544 | tf_op jit(solution)/shard_map/bkgs,ls->bkgl/dot_general | solution.py:26
  6.9 0.5 copy.31
  7.5 0.3 reshape_reshape.2
  7.8 1.6 %copy.32 = f32[1,56,64,64]{3,2,1,0:T(8,128)} copy(f32[1,56,64,64]{3,1,2,0:T(8,128)S(1)} %bitcast.120) | data formatting | bytes 1835008 | tf_op jit(solution)/shard_map/transpose | solution.py:41
  9.4 2.1 %reshape.451 = f32[56,4096]{1,0:T(8,128)S(1)} reshape(f32[1,56,64,64]{3,2,1,0:T(8,128)} %copy.32) | data formatting | bytes 1835008 | tf_op jit(solution)/shard_map/reshape | solution.py:79
  11.4 14.0 %gather_fusion = f32[1792]{0:T(1024)S(1)} fusion(f32[56,4096]{1,0:T(8,128)S(1)} %reshape.451, s32[1792]{0:T(1024)S(1)} %reshape.453), kind=kCustom, calls=%fused_computation | custom fusion | bytes 28672 | tf_op jit(solution)/shard_map/jit(take_along_axis)/gather | solution.py:81
  25.6 0.8 reshape.466
  26.4 7.3 %all-to-all-start = ((f32[8,1,1792]{2,1,0:T(1,128)}), f32[8,1,1792]{2,1,0:T(1,128)}, u32[]{:S(2)}, u32[]{:S(2)}) async-start(f32[8,1,1792]{2,1,0:T(1,128)} %reshape.466), calls=%async_computation | async-start | bytes 114688 | tf_op jit(solution)/shard_map/all_to_all | solution.py:87
  33.8 31.2 %all_gather.3 = f32[8,1,56,32]{2,3,1,0:T(8,128)S(1)} all-gather(f32[1,1,56,32]{2,3,1,0:T(8,128)S(1)} %convert_element_type.28), channel_id=1, replica_groups=mesh['dp'=8,'mp'=4] {'dp'}, dimensions={0}, use_global_device_ids=true | all-gather | bytes 64512 | tf_op jit(solution)/shard_map/all_gather | solution.py:89
  65.1 3.1 %convolution_bitcast_fusion.2 = f32[1,64,56,64]{3,1,2,0:T(8,128)S(1)} fusion(s32[56,32]{1,0:T(8,128)S(1)} %get-tuple-element.5, f32[56,32]{1,0:T(8,128)S(1)} %and_select_fusion, s32[56,32]{1,0:T(8,128)S(1)} %get-tuple-element.4), kind=kOutput, calls=%fused_computation.12 | convolution fusion | flops 88424448 | bytes 939008 | tf_op jit(solution)/shard_map/nbcjk,nbcjl->bckl/dot_general | solution.py:53
  68.2 1.1 copy.34
  69.6 1.5 %convolution_bitcast_fusion.4 = f32[28,8,8,128]{3,2,1,0:T(8,128)S(1)} fusion(f32[128,128,1]{1,0,2:T(8,128)S(1)} %reshape.463, f32[64,28,128]{2,1,0:T(8,128)S(1)} %reshape.447), kind=kOutput, calls=%fused_computation.15 | convolution fusion | flops 352321536 | bytes 1900544 | tf_op jit(solution)/shard_map/bkgl,ls->bkgs/dot_general | solution.py:33
  71.1 2.0 %fusion.2 = f32[1,64,3584]{2,1,0:T(8,128)} fusion(f32[28,8,8,128]{3,2,1,0:T(8,128)S(1)} %convolution_bitcast_fusion.4, bf16[1,64,3584]{2,1,0:T(8,128)(2,1)S(1)} %copy-done.1, f32[1,64,3584]{2,1,0:T(8,128)S(1)} %copy-done, f32[64]{0:T(128)S(1)} %get-tuple-element.9, f32[64]{0:T(128)S(1)} %get-tuple-element.8), kind=kOutput, calls=%fused_computation.7 | convolution fusion | flops 177090560 | bytes 3211776 | tf_op jit(solution)/shard_map/kr,bkf->brf/dot_general | solution.py:35
  73.5 0.5 broadcast.365
  74.0 1.6 %reduce.3 = f32[8,1792]{1,0:T(8,128)S(1)} reduce(f32[8,1,1792]{2,1,0:T(1,128)} %all-to-all-done, f32[]{:T(128)} %broadcast.365), dimensions={1}, to_apply=%all_to_all.3.reduce_sub_computation | reduce | bytes 114692 | tf_op jit(solution)/shard_map/all_to_all | solution.py:87
  75.9 22.1 %fusion.7 = f32[1,64,56,64]{3,1,2,0:T(8,128)S(1)} fusion(s32[8,56,32]{2,0,1:T(8,128)S(1)} %copy.43, f32[8,56,32]{2,0,1:T(8,128)S(1)} %copy.42, s32[8,56,32]{2,0,1:T(8,128)S(1)} %copy.37), kind=kOutput, calls=%fused_computation.13 | convolution fusion | flops 707395584 | bytes 1089536 | tf_op jit(solution)/shard_map/nbcjk,nbcjl->bckl/dot_general | solution.py:53
  98.0 1.1 copy.44
  99.4 1.5 %convolution_bitcast_fusion.3 = f32[28,8,8,128]{3,2,1,0:T(8,128)S(1)} fusion(f32[128,128,1]{1,0,2:T(8,128)S(1)} %reshape.463, f32[64,28,128]{2,1,0:T(8,128)S(1)} %reshape.449), kind=kOutput, calls=%fused_computation.14 | convolution fusion | flops 352321536 | bytes 1900544 | tf_op jit(solution)/shard_map/bkgl,ls->bkgs/dot_general | solution.py:33
  100.9 1.8 %multiply_reduce_fusion = (f32[]{:T(128)}, f32[3584,64]{0,1:T(8,128)S(1)}) fusion(f32[64]{0:T(128)S(1)} %get-tuple-element.9, f32[64]{0:T(128)S(1)} %get-tuple-element.8, f32[28,8,8,128]{3,2,1,0:T(8,128)S(1)} %convolution_bitcast_fusion.3), kind=kOutput, calls=%fused_computation.27 | convolution fusion | flops 176631808 | bytes 1835524 | tf_op jit(solution)/shard_map/kr,bkf->brf/dot_general | solution.py:35
  102.6 6.3 %psum.7 = f32[]{:T(128)} all-reduce(f32[]{:T(128)} %get-tuple-element.6), channel_id=1, replica_groups=mesh['dp'=8,'mp'=4] {'mp'}, use_global_device_ids=true, to_apply=%region_1.2 | all-reduce | flops 1 | bytes 8 | tf_op jit(solution)/shard_map/psum | solution.py:94
  109.6 1.0 bitcast_subtract_fusion
  (33 shorter events, 2.3 us)
Async XLA Ops:
  11.4 22.3 %copy-start.3 = (s32[1,1,56,32]{2,3,1,0:T(8,128)S(1)}, s32[1,1,56,32]{2,3,1,0:T(8,128)}, u32[]{:S(2)}) copy-start(s32[1,1,56,32]{2,3,1,0:T(8,128)} %param.7) | copy-start | bytes 21508
  26.4 47.1 %all-to-all-start = ((f32[8,1,1792]{2,1,0:T(1,128)}), f32[8,1,1792]{2,1,0:T(1,128)}, u32[]{:S(2)}, u32[]{:S(2)}) async-start(f32[8,1,1792]{2,1,0:T(1,128)} %reshape.466), calls=%async_computation | async-start | bytes 114688 | tf_op jit(solution)/shard_map/all_to_all | solution.py:87
  69.2 1.8 %copy-start.1 = (bf16[1,64,3584]{2,1,0:T(8,128)(2,1)S(1)}, bf16[1,64,3584]{2,1,0:T(8,128)(2,1)}, u32[]{:S(2)}) copy-start(bf16[1,64,3584]{2,1,0:T(8,128)(2,1)} %param.4) | copy-start | bytes 1376260
  69.6 1.5 %copy-start = (f32[1,64,3584]{2,1,0:T(8,128)S(1)}, f32[1,64,3584]{2,1,0:T(8,128)}, u32[]{:S(2)}) copy-start(f32[1,64,3584]{2,1,0:T(8,128)} %param.5) | copy-start | bytes 2752516
  100.9 8.7 %copy-start.2 = (f32[64,3584]{1,0:T(8,128)S(1)}, f32[64,3584]{1,0:T(8,128)}, u32[]{:S(2)}) copy-start(f32[64,3584]{1,0:T(8,128)} %param.6) | copy-start | bytes 2752516
